TPU v7x, 32 devices: a whole 2x2x4 slice. The times are simulated.
32 devices in a mesh: row: 8 (over y, x, core), col: 4 (over z).
Axes of the slice: x: 2, y: 2, z: 4, core: 2. Of those that a mesh axis runs over, the one named last changes fastest.
Arguments:
- tokens: bfloat16 [256, 8192], P('row', 'col'), may hold values from -6 to 6
- gate_codes: int32 [1024, 28672], P('col', 'row'), may hold values from -2147483648 to 2147483646
- up_codes: int32 [1024, 28672], P('col', 'row'), may hold values from -2147483648 to 2147483646
- down_codes: int32 [3584, 8192], P('row', 'col'), may hold values from -2147483648 to 2147483646
- gate_scales: bfloat16 [64, 28672], P('row'), may hold values from 0.0009994507 to 0.0049743652
- up_scales: bfloat16 [64, 28672], P('row'), may hold values from 0.0009994507 to 0.0049743652
- down_scales: bfloat16 [8192, 224], P('row'), may hold values from 0.00059890747 to 0.0029907227
Outputs:
- mixed: bfloat16 [256, 8192], P('row', 'col')
Inputs may be any that keep to these rules, and one draw needn't show every extreme that they name: Every word of gate_codes, up_codes and down_codes is an arbitrary 32-bit pattern: all sixteen codes occur in every nibble position.
All inputs are finite; a program needn't handle non-finite values.
Results may differ from a plain program's by a relative error of at most 0.025.
Values may be sent and summed in bfloat16 or wider, within the bound.
A program may use at most 192 MiB of HBM per device.

v0:
```python
import jax
import jax.numpy as jnp
from jax import lax
from jax.experimental import pallas as pl
from jax.experimental.pallas import tpu as pltpu
from jax.sharding import PartitionSpec as P

GROUP = 128
PACK = 8
SUB = GROUP // PACK


def tile_of(width, most):
    tile = (min(width, most) // 128) * 128
    while width % tile:
        tile -= 128
    return tile


def permutation():
    source = lax.broadcasted_iota(jnp.int32, (GROUP, GROUP), 0)
    target = lax.broadcasted_iota(jnp.int32, (GROUP, GROUP), 1)
    wanted = lax.rem(target, SUB) * PACK + lax.div(target, SUB)
    return (source == wanted).astype(jnp.bfloat16)


def permute_features(source_ref, target_ref):
    perm = permutation()
    for group in range(source_ref.shape[1] // GROUP):
        at = pl.ds(group * GROUP, GROUP)
        target_ref[:, at] = jnp.dot(
            source_ref[:, at], perm, preferred_element_type=jnp.float32
        ).astype(jnp.bfloat16)


def dequantize(codes_ref, scales_ref, dense_ref):
    def one(group, carry):
        word = codes_ref[pl.ds(pl.multiple_of(group * SUB, SUB), SUB), :] ^ jnp.int32(-2004318072)
        scale = scales_ref[pl.ds(group, 1), :]
        for k in range(PACK):
            code = word if k == PACK - 1 else jnp.left_shift(word, 28 - 4 * k)
            value = jnp.right_shift(code, 28).astype(jnp.float32)
            row = pl.multiple_of(group * GROUP + k * SUB, SUB)
            dense_ref[pl.ds(row, SUB), :] = (value * scale).astype(jnp.bfloat16)
        return carry

    lax.fori_loop(0, codes_ref.shape[0] // SUB, one, 0)


def up_kernel(tokens, gate, up, gate_scale, up_scale, out, moved, dense):
    @pl.when(pl.program_id(0) == 0)
    def _():
        permute_features(tokens, moved)

    for index, (codes, scale) in enumerate(((gate, gate_scale), (up, up_scale))):
        dequantize(codes, scale, dense.at[index])
        total = jnp.dot(moved[...], dense[index], preferred_element_type=jnp.float32)
        parts, _, rows, width = out.shape
        out[:, index] = total.astype(jnp.bfloat16).reshape(parts, rows, width)


def down_kernel(hidden, codes, scale, out, moved, dense):
    @pl.when(pl.program_id(0) == 0)
    def _():
        permute_features(hidden, moved)

    dequantize(codes, scale, dense)
    out[...] = jnp.dot(moved[...], dense[...], preferred_element_type=jnp.float32).astype(
        jnp.bfloat16
    )


PARAMS = dict(dimension_semantics=("arbitrary",), vmem_limit_bytes=58 * 1024 * 1024)


def project_up(tokens, gate, up, gate_scale, up_scale, parts):
    count, model = tokens.shape
    words, width = gate.shape
    groups = gate_scale.shape[0]
    tile = tile_of(width, 512)
    codes = pl.BlockSpec((words, tile), lambda i: (0, i))
    scales = pl.BlockSpec((groups, tile), lambda i: (0, i))
    return pl.pallas_call(
        up_kernel,
        grid=(width // tile,),
        in_specs=[pl.BlockSpec((count, model), lambda i: (0, 0)), codes, codes, scales, scales],
        out_specs=pl.BlockSpec((parts, 2, count // parts, tile), lambda i: (0, 0, 0, i)),
        out_shape=jax.ShapeDtypeStruct((parts, 2, count // parts, width), jnp.bfloat16),
        scratch_shapes=[
            pltpu.VMEM((count, model), jnp.bfloat16),
            pltpu.VMEM((2, model, tile), jnp.bfloat16),
        ],
        cost_estimate=pl.CostEstimate(
            flops=4 * count * model * width,
            bytes_accessed=8 * words * width,
            transcendentals=0,
        ),
        compiler_params=pltpu.CompilerParams(**PARAMS),
    )(tokens, gate, up, gate_scale, up_scale)


def project_down(hidden, codes, scale):
    count, units = hidden.shape
    words, width = codes.shape
    groups = scale.shape[0]
    tile = tile_of(width, 512)
    return pl.pallas_call(
        down_kernel,
        grid=(width // tile,),
        in_specs=[
            pl.BlockSpec((count, units), lambda i: (0, 0)),
            pl.BlockSpec((words, tile), lambda i: (0, i)),
            pl.BlockSpec((groups, tile), lambda i: (0, i)),
        ],
        out_specs=pl.BlockSpec((count, tile), lambda i: (0, i)),
        out_shape=jax.ShapeDtypeStruct((count, width), jnp.bfloat16),
        scratch_shapes=[
            pltpu.VMEM((count, units), jnp.bfloat16),
            pltpu.VMEM((units, tile), jnp.bfloat16),
        ],
        cost_estimate=pl.CostEstimate(
            flops=2 * count * units * width,
            bytes_accessed=4 * words * width,
            transcendentals=0,
        ),
        compiler_params=pltpu.CompilerParams(**PARAMS),
    )(hidden, codes, scale)


def per_device(tokens, gate_codes, up_codes, down_codes, gate_scales, up_scales, down_scales):
    parts = lax.axis_size("col")
    col = lax.axis_index("col")
    gate_local, up_local, down_local = (
        lax.all_to_all(scales, "row", split_axis=1, concat_axis=0, tiled=True)
        for scales in (gate_scales, up_scales, down_scales)
    )
    groups = gate_local.shape[0] // parts
    gate_part = lax.dynamic_slice_in_dim(gate_local, col * groups, groups, 0).astype(jnp.float32)
    up_part = lax.dynamic_slice_in_dim(up_local, col * groups, groups, 0).astype(jnp.float32)
    width = down_codes.shape[1]
    down_part = lax.dynamic_slice_in_dim(down_local, col * width, width, 0).T.astype(jnp.float32)
    gathered = lax.all_gather(tokens, "row", axis=0, tiled=True)
    sums = project_up(gathered, gate_codes, up_codes, gate_part, up_part, parts)
    mine = lax.psum_scatter(sums, "col", scatter_dimension=0, tiled=True)[0].astype(jnp.float32)
    hidden = (jax.nn.silu(mine[0]) * mine[1]).astype(jnp.bfloat16)
    hidden = lax.all_gather(hidden, "col", axis=0, tiled=True)
    partial = project_down(hidden, down_codes, down_part)
    return lax.psum_scatter(partial, "row", scatter_dimension=0, tiled=True)


def solution(mesh):
    placed = (
        P("row", "col"),
        P("col", "row"),
        P("col", "row"),
        P("row", "col"),
        P("row", None),
        P("row", None),
        P("row", None),
    )
    return jax.shard_map(
        per_device, mesh=mesh, in_specs=placed, out_specs=P("row", "col"), check_vma=False
    )
```

profile of v0, /device:TPU:0, one launch (start us, length us, event | category | flops | bytes accessed | tf_op | source)
XLA Modules:
  0.0 228.7 jit_solution(4968411089961897337)
XLA Ops:
  6.5 0.0 all-gather.3.cloned.1.call-start
  6.5 0.7 all-gather.3.cloned.1.call-update
  7.3 5.2 %all-to-all-start.1 = ((bf16[8,8,3584]{2,0,1:T(8,128)(2,1)}), bf16[8,8,3584]{2,0,1:T(8,128)(2,1)S(1)}, u32[]{:S(2)}, u32[]{:S(2)}) async-start(bf16[8,8,3584]{2,0,1:T(8,128)(2,1)} %bitcast.36), calls=%async_computation.1 | async-start | bytes 917504 | tf_op jit(solution)/shard_map/all_to_all | solution.py:134
  12.5 9.0 %all-to-all-done.1 = bf16[8,8,3584]{2,0,1:T(8,128)(2,1)S(1)} async-done(((bf16[8,8,3584]{2,0,1:T(8,128)(2,1)}), bf16[8,8,3584]{2,0,1:T(8,128)(2,1)S(1)}, u32[]{:S(2)}, u32[]{:S(2)}) %all-to-all-start.1) | async-done | bytes 458784 | tf_op jit(solution)/shard_map/all_to_all | solution.py:134
  21.5 3.5 %all-to-all-start = ((bf16[8,8,3584]{2,0,1:T(8,128)(2,1)}), bf16[8,8,3584]{2,0,1:T(8,128)(2,1)S(1)}, u32[]{:S(2)}, u32[]{:S(2)}) async-start(bf16[8,8,3584]{2,0,1:T(8,128)(2,1)} %bitcast.37), calls=%async_computation | async-start | bytes 917504 | tf_op jit(solution)/shard_map/all_to_all | solution.py:134
  25.0 0.0 reduce-scatter.3.cloned.1.call-start
  25.0 0.7 dynamic-slice_convert_fusion.up_scale
  25.7 10.7 %all-to-all-done = bf16[8,8,3584]{2,0,1:T(8,128)(2,1)S(1)} async-done(((bf16[8,8,3584]{2,0,1:T(8,128)(2,1)}), bf16[8,8,3584]{2,0,1:T(8,128)(2,1)S(1)}, u32[]{:S(2)}, u32[]{:S(2)}) %all-to-all-start) | async-done | bytes 458784 | tf_op jit(solution)/shard_map/all_to_all | solution.py:134
  36.4 0.7 dynamic-slice_convert_fusion.1.gate_scale
  37.1 0.2 all-gather.3.cloned.1.call-done.tokens
  37.3 23.7 %shard_map.73 = bf16[4,2,64,3584]{3,2,1,0:T(8,128)(2,1)} custom-call(bf16[256,2048]{1,0:T(8,128)(2,1)} %all-gather.3.cloned.1.call-done.tokens, s32[256,3584]{1,0:T(8,128)} %gate.1, s32[256,3584]{1,0:T(8,128)} %up.1, f32[16,3584]{1,0:T(8,128)} %dynamic-slice_convert_fusion.1.gate_scale, f32[16,3584]{1,0:T(8,128)} %dynamic-slice_convert_fusion.up_scale), custom_call_target="tpu_custom_call" | custom-call | flops 7516192768 | bytes 7340032 | tf_op jit(solution)/shard_map/pallas_call | solution.py:83
  60.9 0.0 reduce-scatter.3.cloned.1.call-update
  60.9 0.0 copy-start
  61.0 0.0 all-gather.5.cloned.1.call-start
  61.0 69.0 %reduce-scatter.3.cloned.1.call-done = bf16[1,2,64,3584]{3,2,1,0:T(8,128)(2,1)} async-done(((bf16[4,2,64,3584]{3,2,1,0:T(8,128)(2,1)}), bf16[1,2,64,3584]{3,2,1,0:T(8,128)(2,1)}) %reduce-scatter.3.cloned.1.call-update) | async-done | bytes 917520 | tf_op jit(solution)/shard_map/reduce_scatter | solution.py:144
  130.0 1.4 convert_element_type.20
  131.3 1.0 fusion.1
  132.4 0.0 all-gather.5.cloned.1.call-update
  132.4 0.0 copy-done
  132.4 0.9 all_to_all.50
  133.3 3.6 %all-to-all-start.2 = ((bf16[1024,8,28]{0,2,1:T(8,128)(2,1)}), bf16[1024,8,28]{0,2,1:T(8,128)(2,1)S(1)}, u32[]{:S(2)}, u32[]{:S(2)}) async-start(bf16[1024,8,28]{0,2,1:T(8,128)(2,1)} %all_to_all.50), calls=%async_computation.3 | async-start | bytes 1048576 | tf_op jit(solution)/shard_map/all_to_all | solution.py:134
  136.9 0.0 reduce-scatter.5.cloned.1.call-start
  137.0 9.7 %all-to-all-done.2 = bf16[1024,8,28]{0,2,1:T(8,128)(2,1)S(1)} async-done(((bf16[1024,8,28]{0,2,1:T(8,128)(2,1)}), bf16[1024,8,28]{0,2,1:T(8,128)(2,1)S(1)}, u32[]{:S(2)}, u32[]{:S(2)}) %all-to-all-start.2) | async-done | bytes 458784 | tf_op jit(solution)/shard_map/all_to_all | solution.py:134
  146.6 0.3 copy.12
  146.9 0.3 copy.10
  147.3 0.7 convert_bitcast_fusion.scale
  148.0 26.1 %all-gather.5.cloned.1.call-done.hidden = bf16[256,3584]{1,0:T(8,128)(2,1)} async-done(((bf16[64,3584]{1,0:T(8,128)(2,1)}), bf16[256,3584]{1,0:T(8,128)(2,1)}) %all-gather.5.cloned.1.call-update) | async-done | bytes 1835024 | tf_op jit(solution)/shard_map/all_gather | solution.py:146
  174.1 13.0 %shard_map.74 = bf16[256,2048]{1,0:T(8,128)(2,1)} custom-call(bf16[256,3584]{1,0:T(8,128)(2,1)} %all-gather.5.cloned.1.call-done.hidden, s32[448,2048]{1,0:T(8,128)} %codes.1, f32[28,2048]{1,0:T(8,128)} %convert_bitcast_fusion.scale), custom_call_target="tpu_custom_call" | custom-call | flops 3758096384 | bytes 3670016 | tf_op jit(solution)/shard_map/pallas_call | solution.py:107
  187.1 0.0 reduce-scatter.5.cloned.1.call-update
  187.1 35.0 %reduce-scatter.5.cloned.1.call-done = bf16[32,2048]{1,0:T(8,128)(2,1)} async-done(((bf16[256,2048]{1,0:T(8,128)(2,1)}), bf16[32,2048]{1,0:T(8,128)(2,1)}) %reduce-scatter.5.cloned.1.call-update) | async-done | bytes 131088 | tf_op jit(solution)/shard_map/reduce_scatter | solution.py:148
  (1 shorter events, 0.0 us)
Async XLA Ops:
  6.5 30.7 %all-gather.3.cloned.1.call-start = ((), (), s32[]{:S(2)}) async-start(), calls=%async_computation.5 | async-start | bytes 1179648 | tf_op jit(solution)/shard_map/all_gather | solution.py:142
  7.3 14.2 %all-to-all-start.1 = ((bf16[8,8,3584]{2,0,1:T(8,128)(2,1)}), bf16[8,8,3584]{2,0,1:T(8,128)(2,1)S(1)}, u32[]{:S(2)}, u32[]{:S(2)}) async-start(bf16[8,8,3584]{2,0,1:T(8,128)(2,1)} %bitcast.36), calls=%async_computation.1 | async-start | bytes 917504 | tf_op jit(solution)/shard_map/all_to_all | solution.py:134
  21.5 14.9 %all-to-all-start = ((bf16[8,8,3584]{2,0,1:T(8,128)(2,1)}), bf16[8,8,3584]{2,0,1:T(8,128)(2,1)S(1)}, u32[]{:S(2)}, u32[]{:S(2)}) async-start(bf16[8,8,3584]{2,0,1:T(8,128)(2,1)} %bitcast.37), calls=%async_computation | async-start | bytes 917504 | tf_op jit(solution)/shard_map/all_to_all | solution.py:134
  25.0 105.0 %reduce-scatter.3.cloned.1.call-start = ((), (), s32[]{:S(2)}) async-start(), calls=%async_computation.6 | async-start | bytes 4587520 | tf_op jit(solution)/shard_map/reduce_scatter | solution.py:144
  60.9 71.4 %copy-start = (bf16[1024,224]{0,1:T(8,128)(2,1)S(1)}, bf16[1024,224]{0,1:T(8,128)(2,1)}, u32[]{:S(2)}) copy-start(bf16[1024,224]{0,1:T(8,128)(2,1)} %param.13) | copy-start | bytes 1376260
  61.0 113.2 %all-gather.5.cloned.1.call-start = ((), (), s32[]{:S(2)}) async-start(), calls=%async_computation.7 | async-start | bytes 2293760 | tf_op jit(solution)/shard_map/all_gather | solution.py:146
  133.3 13.4 %all-to-all-start.2 = ((bf16[1024,8,28]{0,2,1:T(8,128)(2,1)}), bf16[1024,8,28]{0,2,1:T(8,128)(2,1)S(1)}, u32[]{:S(2)}, u32[]{:S(2)}) async-start(bf16[1024,8,28]{0,2,1:T(8,128)(2,1)} %all_to_all.50), calls=%async_computation.3 | async-start | bytes 1048576 | tf_op jit(solution)/shard_map/all_to_all | solution.py:134
  136.9 85.2 %reduce-scatter.5.cloned.1.call-start = ((), (), s32[]{:S(2)}) async-start(), calls=%async_computation.8 | async-start | bytes 1179648 | tf_op jit(solution)/shard_map/reduce_scatter | solution.py:148
Sparse Core Ops, SparseCore 0:
  9.2 27.9 all-gather.2
  61.1 68.8 reduce-scatter.2
  132.5 41.5 all-gather.4
  187.3 34.8 reduce-scatter.4
where the time goes:
time: 229 us
  waiting for transfers between devices  160 us (70%)
  Pallas kernels  36.7 us (16%)
  between operations  13.2 us (6%)
  starting transfers between devices  12.5 us (5%)
  other arithmetic  4.54 us (2%)
    reduce_scatter x1, waiting for transfers between devices, per_device(): lax.psum_scatter(sums, 'col', scatter_dimension=0, tiled=True)[0]  69 us
    reduce_scatter x1, waiting for transfers between devices, per_device(): return lax.psum_scatter(partial, 'row', scatter_dimension=0, tiled=True)  35 us
    all_to_all x3, waiting for transfers between devices, per_device(): lax.all_to_all(scales, 'row', split_axis=1, concat_axis=0, tiled=True)  29.3 us
    all_gather x1, waiting for transfers between devices, per_device(): hidden = lax.all_gather(hidden, 'col', axis=0, tiled=True)  26.1 us
    pallas_call x1, Pallas kernels, project_up(): pl.pallas_call(up_kernel, grid=(width // tile,), in_specs=[pl.BlockSpec((...  23.7 us
    pallas_call x1, Pallas kernels, project_down(): pl.pallas_call(down_kernel, grid=(width // tile,), in_specs=[pl.BlockSpec...  13 us
    all_to_all x3, starting transfers between devices, per_device(): lax.all_to_all(scales, 'row', split_axis=1, concat_axis=0, tiled=True)  12.3 us
  transfers between devices with their start and end apart: 7, of which 7 were waited for; matrix products, arithmetic and copies ran while one was open for 1% of the time, Pallas kernels for 0%

commit v1 on v0

--- a/solution.py
+++ b/solution.py
@@ -1,3 +1,5 @@
+import functools
+
 import jax
 import jax.numpy as jnp
 from jax import lax
@@ -55,8 +57,7 @@
     for index, (codes, scale) in enumerate(((gate, gate_scale), (up, up_scale))):
         dequantize(codes, scale, dense.at[index])
         total = jnp.dot(moved[...], dense[index], preferred_element_type=jnp.float32)
-        parts, _, rows, width = out.shape
-        out[:, index] = total.astype(jnp.bfloat16).reshape(parts, rows, width)
+        out[index] = total.astype(jnp.bfloat16)
 
 
 def down_kernel(hidden, codes, scale, out, moved, dense):
@@ -73,7 +74,7 @@
 PARAMS = dict(dimension_semantics=("arbitrary",), vmem_limit_bytes=58 * 1024 * 1024)
 
 
-def project_up(tokens, gate, up, gate_scale, up_scale, parts):
+def project_up(tokens, gate, up, gate_scale, up_scale):
     count, model = tokens.shape
     words, width = gate.shape
     groups = gate_scale.shape[0]
@@ -84,8 +85,8 @@
         up_kernel,
         grid=(width // tile,),
         in_specs=[pl.BlockSpec((count, model), lambda i: (0, 0)), codes, codes, scales, scales],
-        out_specs=pl.BlockSpec((parts, 2, count // parts, tile), lambda i: (0, 0, 0, i)),
-        out_shape=jax.ShapeDtypeStruct((parts, 2, count // parts, width), jnp.bfloat16),
+        out_specs=pl.BlockSpec((2, count, tile), lambda i: (0, 0, i)),
+        out_shape=jax.ShapeDtypeStruct((2, count, width), jnp.bfloat16),
         scratch_shapes=[
             pltpu.VMEM((count, model), jnp.bfloat16),
             pltpu.VMEM((2, model, tile), jnp.bfloat16),
@@ -127,25 +128,279 @@
     )(hidden, codes, scale)
 
 
+VMEM_REF = pl.BlockSpec(memory_space=pltpu.VMEM)
+MESH = pl.DeviceIdType.MESH
+DMA = pltpu.SemaphoreType.DMA
+REMOTE = pltpu.CompilerParams(has_side_effects=True, vmem_limit_bytes=58 * 1024 * 1024)
+
+
+def gather_kernel(
+    rows, share, tokens, gate, up, down, all_tokens, gate_out, up_out, down_out,
+    gate_got, up_got, down_got, token_send, token_recv, scale_send, scale_recv,
+):
+    row, col = lax.axis_index("row"), lax.axis_index("col")
+    count, width = tokens.shape[0], gate_got.shape[2]
+    home, slot = lax.div(row, share), lax.rem(row, share)
+    mine = pl.ds(pl.multiple_of(row * count, count), count)
+
+    def token_copy(step):
+        return pltpu.make_async_remote_copy(
+            src_ref=tokens,
+            dst_ref=all_tokens.at[mine],
+            send_sem=token_send.at[step],
+            recv_sem=token_recv.at[step],
+            device_id={"row": lax.rem(row + step, rows), "col": col},
+            device_id_type=MESH,
+        )
+
+    def scale_copies(j, at, peer_row, peer_col):
+        columns = pl.ds(pl.multiple_of((col * share + j) * width, 128), width)
+        pairs = (
+            (gate.at[:, columns], gate_got.at[at]),
+            (up.at[:, columns], up_got.at[at]),
+            (down.at[col * share + j], down_got.at[at]),
+        )
+        return pairs, [
+            pltpu.make_async_remote_copy(
+                src_ref=source,
+                dst_ref=target,
+                send_sem=scale_send.at[kind, j],
+                recv_sem=scale_recv.at[kind, at],
+                device_id={"row": peer_row, "col": peer_col},
+                device_id_type=MESH,
+            )
+            for kind, (source, target) in enumerate(pairs)
+        ]
+
+    for j in range(share):
+        peer = col * share + j
+        pairs, copies = scale_copies(j, slot, peer, home)
+        here = jnp.logical_and(peer == row, home == col)
+
+        @pl.when(jnp.logical_not(here))
+        def _():
+            for copy in copies:
+                copy.start()
+
+        @pl.when(here)
+        def _():
+            for source, target in pairs:
+                target[...] = source[...]
+
+    for step in range(rows - 1, 0, -1):
+        token_copy(step).start()
+    all_tokens[mine] = tokens[...]
+
+    other = lax.rem(row + 1, rows)
+    for t in range(share):
+        @pl.when(col * share + t != row)
+        def _():
+            for copy in scale_copies(0, t, other, col)[1]:
+                copy.wait_recv()
+
+    lines, span = gate_got.shape[1], down_got.shape[2]
+    for t in range(share):
+        gate_out[t * lines : (t + 1) * lines] = gate_got[t].astype(jnp.float32)
+        up_out[t * lines : (t + 1) * lines] = up_got[t].astype(jnp.float32)
+        down_out[:, t * span : (t + 1) * span] = down_got[t].astype(jnp.float32)
+    for step in range(1, rows):
+        token_copy(step).wait()
+    for j in range(share):
+        peer = col * share + j
+
+        @pl.when(jnp.logical_not(jnp.logical_and(peer == row, home == col)))
+        def _():
+            for copy in scale_copies(j, slot, peer, home)[1]:
+                copy.wait_send()
+
+
+def gather(tokens, gate, up, down, rows, cols):
+    count, model = tokens.shape
+    lines = gate.shape[0]
+    width = gate.shape[1] // rows
+    groups, span = down.shape[0] // rows, down.shape[1]
+    share = rows // cols
+    down = down.reshape(rows, groups, span)
+    return pl.pallas_call(
+        functools.partial(gather_kernel, rows, share),
+        in_specs=[VMEM_REF] * 4,
+        out_specs=[VMEM_REF] * 4,
+        out_shape=[
+            jax.ShapeDtypeStruct((count * rows, model), jnp.bfloat16),
+            jax.ShapeDtypeStruct((share * lines, width), jnp.float32),
+            jax.ShapeDtypeStruct((share * lines, width), jnp.float32),
+            jax.ShapeDtypeStruct((groups, share * span), jnp.float32),
+        ],
+        scratch_shapes=[
+            pltpu.VMEM((share, lines, width), jnp.bfloat16),
+            pltpu.VMEM((share, lines, width), jnp.bfloat16),
+            pltpu.VMEM((share, groups, span), jnp.bfloat16),
+            DMA((rows,)),
+            DMA((rows,)),
+            DMA((3, share)),
+            DMA((3, share)),
+        ],
+        compiler_params=REMOTE,
+        name="gather",
+    )(tokens, gate, up, down)
+
+
+def chain_kernel(cols, chunks, sums, hidden, got, sum_send, sum_recv, hid_send, hid_recv):
+    col = lax.axis_index("col")
+    last = cols - 1
+    half = sums.shape[1] // 2
+    depth = half // chunks
+    before, after = jnp.maximum(col - 1, 0), jnp.minimum(col + 1, last)
+    any_peer = jnp.where(col == last, col - 1, col + 1)
+    sides = ((last, 0, before, after), (0, last, after, before))
+
+    def rows_of(side, q):
+        return pl.ds(side * half + q * depth, depth)
+
+    def sum_copy(side, q, source, peer):
+        return pltpu.make_async_remote_copy(
+            src_ref=source,
+            dst_ref=got.at[side, q],
+            send_sem=sum_send.at[side, q],
+            recv_sem=sum_recv.at[side, q],
+            device_id={"col": peer},
+            device_id_type=MESH,
+        )
+
+    def hid_copy(side, q, peer):
+        return pltpu.make_async_remote_copy(
+            src_ref=hidden.at[rows_of(side, q)],
+            dst_ref=hidden.at[rows_of(side, q)],
+            send_sem=hid_send.at[side, q],
+            recv_sem=hid_recv.at[side, q],
+            device_id={"col": peer},
+            device_id_type=MESH,
+        )
+
+    for side, (first, end, down_peer, up_peer) in enumerate(sides):
+        @pl.when(col == first)
+        def _():
+            for q in range(chunks):
+                sum_copy(side, q, sums.at[:, rows_of(side, q)], down_peer).start()
+
+    for q in range(chunks):
+        for side, (first, end, down_peer, up_peer) in enumerate(sides):
+            @pl.when(col != first)
+            def _():
+                sum_copy(side, q, got.at[side, q], any_peer).wait_recv()
+                total = got[side, q].astype(jnp.float32) + sums[:, rows_of(side, q)].astype(
+                    jnp.float32
+                )
+
+                @pl.when(col != end)
+                def _():
+                    got[side, q] = total.astype(jnp.bfloat16)
+                    sum_copy(side, q, got.at[side, q], down_peer).start()
+
+                @pl.when(col == end)
+                def _():
+                    value = jax.nn.silu(total[0]) * total[1]
+                    hidden[rows_of(side, q)] = value.astype(jnp.bfloat16)
+                    hid_copy(side, q, up_peer).start()
+
+    for q in range(chunks):
+        for side, (first, end, down_peer, up_peer) in enumerate(sides):
+            @pl.when(col != end)
+            def _():
+                hid_copy(side, q, any_peer).wait_recv()
+
+                @pl.when(col != first)
+                def _():
+                    hid_copy(side, q, up_peer).start()
+
+    for q in range(chunks):
+        for side, (first, end, down_peer, up_peer) in enumerate(sides):
+            @pl.when(col != end)
+            def _():
+                sum_copy(side, q, got.at[side, q], any_peer).wait_send()
+
+            @pl.when(col != first)
+            def _():
+                hid_copy(side, q, any_peer).wait_send()
+
+
+def chain(sums, cols):
+    _, count, width = sums.shape
+    chunks = 8
+    while count % (2 * 16 * chunks):
+        chunks //= 2
+    depth = count // (2 * chunks)
+    return pl.pallas_call(
+        functools.partial(chain_kernel, cols, chunks),
+        in_specs=[VMEM_REF],
+        out_specs=VMEM_REF,
+        out_shape=jax.ShapeDtypeStruct((count, width), jnp.bfloat16),
+        scratch_shapes=[
+            pltpu.VMEM((2, chunks, 2, depth, width), jnp.bfloat16),
+            DMA((2, chunks)),
+            DMA((2, chunks)),
+            DMA((2, chunks)),
+            DMA((2, chunks)),
+        ],
+        compiler_params=REMOTE,
+        name="chain",
+    )(sums)
+
+
+def scatter_kernel(rows, partial, out, got, send, recv):
+    row = lax.axis_index("row")
+    count = out.shape[0]
+
+    def block(index):
+        return pl.ds(pl.multiple_of(index * count, count), count)
+
+    def copy(step):
+        peer = lax.rem(row + step, rows)
+        return pltpu.make_async_remote_copy(
+            src_ref=partial.at[block(peer)],
+            dst_ref=got.at[step - 1],
+            send_sem=send.at[step - 1],
+            recv_sem=recv.at[step - 1],
+            device_id={"row": peer},
+            device_id_type=MESH,
+        )
+
+    for step in range(rows - 1, 0, -1):
+        copy(step).start()
+    total = partial[block(row)].astype(jnp.float32)
+    for step in range(rows - 1, 0, -1):
+        copy(step).wait_recv()
+        total = total + got[step - 1].astype(jnp.float32)
+    out[...] = total.astype(jnp.bfloat16)
+    for step in range(1, rows):
+        copy(step).wait_send()
+
+
+def scatter(partial, rows):
+    count, width = partial.shape
+    return pl.pallas_call(
+        functools.partial(scatter_kernel, rows),
+        in_specs=[VMEM_REF],
+        out_specs=VMEM_REF,
+        out_shape=jax.ShapeDtypeStruct((count // rows, width), jnp.bfloat16),
+        scratch_shapes=[
+            pltpu.VMEM((rows - 1, count // rows, width), jnp.bfloat16),
+            DMA((rows - 1,)),
+            DMA((rows - 1,)),
+        ],
+        compiler_params=REMOTE,
+        name="scatter",
+    )(partial)
+
+
 def per_device(tokens, gate_codes, up_codes, down_codes, gate_scales, up_scales, down_scales):
-    parts = lax.axis_size("col")
-    col = lax.axis_index("col")
-    gate_local, up_local, down_local = (
-        lax.all_to_all(scales, "row", split_axis=1, concat_axis=0, tiled=True)
-        for scales in (gate_scales, up_scales, down_scales)
+    rows, cols = lax.axis_size("row"), lax.axis_size("col")
+    gathered, gate_part, up_part, down_part = gather(
+        tokens, gate_scales, up_scales, down_scales.T, rows, cols
     )
-    groups = gate_local.shape[0] // parts
-    gate_part = lax.dynamic_slice_in_dim(gate_local, col * groups, groups, 0).astype(jnp.float32)
-    up_part = lax.dynamic_slice_in_dim(up_local, col * groups, groups, 0).astype(jnp.float32)
-    width = down_codes.shape[1]
-    down_part = lax.dynamic_slice_in_dim(down_local, col * width, width, 0).T.astype(jnp.float32)
-    gathered = lax.all_gather(tokens, "row", axis=0, tiled=True)
-    sums = project_up(gathered, gate_codes, up_codes, gate_part, up_part, parts)
-    mine = lax.psum_scatter(sums, "col", scatter_dimension=0, tiled=True)[0].astype(jnp.float32)
-    hidden = (jax.nn.silu(mine[0]) * mine[1]).astype(jnp.bfloat16)
-    hidden = lax.all_gather(hidden, "col", axis=0, tiled=True)
-    partial = project_down(hidden, down_codes, down_part)
-    return lax.psum_scatter(partial, "row", scatter_dimension=0, tiled=True)
+    sums = project_up(gathered, gate_codes, up_codes, gate_part, up_part)
+    hidden = chain(sums, cols)
+    return scatter(project_down(hidden, down_codes, down_part), rows)
 
 
 def solution(mesh):

time: 229 us -> 276 us (1.21)
  Pallas kernels: 36.7 us -> 272 us
  waiting for transfers between devices: 160 us -> 0 us
  between operations: 13.2 us -> 0.03 us
  starting transfers between devices: 12.5 us -> 0 us
  other arithmetic: 4.54 us -> 0 us
    pallas_call x0 -> x3, Pallas kernels: none -> 236 us  [the longest x1 178 us: chain(): pl.pallas_call(functools.partial(chain_kernel, cols, chunks), in_specs=[V...]
    reduce_scatter x2 -> x0, waiting for transfers between devices: 104 us -> none  [the longest x1 69 us: per_device(): lax.psum_scatter(sums, 'col', scatter_dimension=0, tiled=True)[0]]
    all_to_all x3 -> x0, waiting for transfers between devices: 29.3 us -> none  [per_device(): lax.all_to_all(scales, 'row', split_axis=1, concat_axis=0, tiled=True)]
    all_gather x2 -> x0, waiting for transfers between devices: 26.3 us -> none  [the longest x1 26.1 us: per_device(): hidden = lax.all_gather(hidden, 'col', axis=0, tiled=True)]
    all_to_all x3 -> x0, starting transfers between devices: 12.3 us -> none  [per_device(): lax.all_to_all(scales, 'row', split_axis=1, concat_axis=0, tiled=True)]
    convert_element_type x5 -> x0, other arithmetic: 4.54 us -> none  [the longest x1 1.35 us: per_device(): lax.psum_scatter(sums, 'col', scatter_dimension=0, tiled=True)[0]]
  transfers between devices with their start and end apart: 7 -> 0, of which waited for: 7 -> 0; matrix products, arithmetic and copies ran while one was open for 1% -> 0% of each run, Pallas kernels for 0% -> 0%
where the time goes in v1:
time: 276 us
  Pallas kernels  272 us (99%)
  local copies, waits for them, and re-layouts  3.46 us (1%)
    pallas_call x1, Pallas kernels, chain(): pl.pallas_call(functools.partial(chain_kernel, cols, chunks), in_specs=[V...  178 us
    pallas_call x1, Pallas kernels, gather(): pl.pallas_call(functools.partial(gather_kernel, rows, share), in_specs=[V...  37.5 us
    pallas_call x1, Pallas kernels, project_up(): pl.pallas_call(up_kernel, grid=(width // tile,), in_specs=[pl.BlockSpec((...  23.7 us
    pallas_call x1, Pallas kernels, scatter(): pl.pallas_call(functools.partial(scatter_kernel, rows), in_specs=[VMEM_RE...  19.6 us
    pallas_call x1, Pallas kernels, project_down(): pl.pallas_call(down_kernel, grid=(width // tile,), in_specs=[pl.BlockSpec...  13 us

profile of v1, /device:TPU:0, one launch (start us, length us, event | category | flops | bytes accessed | tf_op | source)
XLA Modules:
  0.0 275.7 jit_solution(5279716872119650213)
XLA Ops:
  0.0 1.9 reshape.3.down
  1.9 37.5 %gather.1 = (bf16[256,2048]{1,0:T(8,128)(2,1)}, f32[16,3584]{1,0:T(8,128)}, f32[16,3584]{1,0:T(8,128)}, f32[28,2048]{1,0:T(8,128)}) custom-call(bf16[32,2048]{1,0:T(8,128)(2,1)} %tokens.1, bf16[8,28672]{1,0:T(8,128)(2,1)} %gate.2, bf16[8,28672]{1,0:T(8,128)(2,1)} %up.2, bf16[8,28,1024]{2,1,0:T(8,128)(2,1)} %reshape.3.down), custom_call_target="tpu_custom_call" | custom-call | tf_op jit(solution)/shard_map/gather/pallas_call | solution.py:224
  39.4 23.7 %shard_map.73.sums = bf16[2,256,3584]{2,1,0:T(8,128)(2,1)} custom-call(bf16[256,2048]{1,0:T(8,128)(2,1)} %get-tuple-element.9.tokens, s32[256,3584]{1,0:T(8,128)} %gate.3, s32[256,3584]{1,0:T(8,128)} %up.3, f32[16,3584]{1,0:T(8,128)} %get-tuple-element.10.gate_scale, f32[16,3584]{1,0:T(8,128)} %get-tuple-element.11.up_scale), custom_call_target="tpu_custom_call" | custom-call | flops 7516192768 | bytes 7340032 | tf_op jit(solution)/shard_map/pallas_call | solution.py:84
  63.1 178.4 %chain.1.hidden = bf16[256,3584]{1,0:T(8,128)(2,1)} custom-call(bf16[2,256,3584]{2,1,0:T(8,128)(2,1)} %shard_map.73.sums), custom_call_target="tpu_custom_call" | custom-call | tf_op jit(solution)/shard_map/chain/pallas_call | solution.py:333
  241.5 13.0 %shard_map.74.partial = bf16[256,2048]{1,0:T(8,128)(2,1)} custom-call(bf16[256,3584]{1,0:T(8,128)(2,1)} %chain.1.hidden, s32[448,2048]{1,0:T(8,128)} %codes.1, f32[28,2048]{1,0:T(8,128)} %get-tuple-element.12.scale), custom_call_target="tpu_custom_call" | custom-call | flops 3758096384 | bytes 3670016 | tf_op jit(solution)/shard_map/pallas_call | solution.py:108
  254.5 19.6 %scatter.1 = bf16[32,2048]{1,0:T(8,128)(2,1)} custom-call(bf16[256,2048]{1,0:T(8,128)(2,1)} %shard_map.74.partial), custom_call_target="tpu_custom_call" | custom-call | tf_op jit(solution)/shard_map/scatter/pallas_call | solution.py:381
  274.1 1.6 copy.9

commit v2 on v1

--- a/solution.py
+++ b/solution.py
@@ -135,30 +135,43 @@
 
 
 def gather_kernel(
-    rows, share, tokens, gate, up, down, all_tokens, gate_out, up_out, down_out,
+    rows, cols, share, tokens, gate, up, down, all_tokens, gate_out, up_out, down_out,
     gate_got, up_got, down_got, token_send, token_recv, scale_send, scale_recv,
 ):
     row, col = lax.axis_index("row"), lax.axis_index("col")
     count, width = tokens.shape[0], gate_got.shape[2]
     home, slot = lax.div(row, share), lax.rem(row, share)
-    mine = pl.ds(pl.multiple_of(row * count, count), count)
-
-    def token_copy(step):
+    group = lax.rem(col - home + cols, cols)
+    sibling = row + 1 - 2 * lax.rem(row, 2)
+
+    def block(owner):
+        return pl.ds(pl.multiple_of(owner * count, count), count)
+
+    def token_copy(step, peer, source, owner):
         return pltpu.make_async_remote_copy(
-            src_ref=tokens,
-            dst_ref=all_tokens.at[mine],
+            src_ref=source,
+            dst_ref=all_tokens.at[block(owner)],
             send_sem=token_send.at[step],
             recv_sem=token_recv.at[step],
-            device_id={"row": lax.rem(row + step, rows), "col": col},
+            device_id={"row": peer, "col": col},
             device_id_type=MESH,
         )
 
+    def own(step):
+        return token_copy(step, lax.rem(row + step, rows), tokens, row)
+
+    def relay(step):
+        owner = lax.rem(row - step + rows, rows)
+        return token_copy(step + 1, sibling, all_tokens.at[block(owner)], owner)
+
+    to_sibling = token_copy(1, sibling, tokens, row)
+
     def scale_copies(j, at, peer_row, peer_col):
-        columns = pl.ds(pl.multiple_of((col * share + j) * width, 128), width)
+        columns = pl.ds(pl.multiple_of((group * share + j) * width, 128), width)
         pairs = (
             (gate.at[:, columns], gate_got.at[at]),
             (up.at[:, columns], up_got.at[at]),
-            (down.at[col * share + j], down_got.at[at]),
+            (down.at[group * share + j], down_got.at[at]),
         )
         return pairs, [
             pltpu.make_async_remote_copy(
@@ -173,7 +186,7 @@
         ]
 
     for j in range(share):
-        peer = col * share + j
+        peer = group * share + j
         pairs, copies = scale_copies(j, slot, peer, home)
         here = jnp.logical_and(peer == row, home == col)
 
@@ -187,13 +200,18 @@
             for source, target in pairs:
                 target[...] = source[...]
 
-    for step in range(rows - 1, 0, -1):
-        token_copy(step).start()
-    all_tokens[mine] = tokens[...]
+    for step in range(rows - 2, 0, -2):
+        own(step).start()
+    to_sibling.start()
+    all_tokens[block(row)] = tokens[...]
+    for step in range(rows - 2, 0, -2):
+        own(step).wait_recv()
+        relay(step).start()
 
     other = lax.rem(row + 1, rows)
+    from_col = lax.rem(col + lax.div(row, share), cols)
     for t in range(share):
-        @pl.when(col * share + t != row)
+        @pl.when(jnp.logical_or(col * share + t != row, from_col != col))
         def _():
             for copy in scale_copies(0, t, other, col)[1]:
                 copy.wait_recv()
@@ -203,10 +221,12 @@
         gate_out[t * lines : (t + 1) * lines] = gate_got[t].astype(jnp.float32)
         up_out[t * lines : (t + 1) * lines] = up_got[t].astype(jnp.float32)
         down_out[:, t * span : (t + 1) * span] = down_got[t].astype(jnp.float32)
-    for step in range(1, rows):
-        token_copy(step).wait()
+    to_sibling.wait()
+    for step in range(2, rows, 2):
+        own(step).wait_send()
+        relay(step).wait()
     for j in range(share):
-        peer = col * share + j
+        peer = group * share + j
 
         @pl.when(jnp.logical_not(jnp.logical_and(peer == row, home == col)))
         def _():
@@ -222,7 +242,7 @@
     share = rows // cols
     down = down.reshape(rows, groups, span)
     return pl.pallas_call(
-        functools.partial(gather_kernel, rows, share),
+        functools.partial(gather_kernel, rows, cols, share),
         in_specs=[VMEM_REF] * 4,
         out_specs=[VMEM_REF] * 4,
         out_shape=[
@@ -255,7 +275,7 @@
     sides = ((last, 0, before, after), (0, last, after, before))
 
     def rows_of(side, q):
-        return pl.ds(side * half + q * depth, depth)
+        return pl.ds(pl.multiple_of(side * half + q * depth, depth), depth)
 
     def sum_copy(side, q, source, peer):
         return pltpu.make_async_remote_copy(
@@ -283,9 +303,11 @@
             for q in range(chunks):
                 sum_copy(side, q, sums.at[:, rows_of(side, q)], down_peer).start()
 
-    for q in range(chunks):
+    def sum_step(step, carry):
         for side, (first, end, down_peer, up_peer) in enumerate(sides):
-            @pl.when(col != first)
+            q = step - (jnp.abs(col - first) - 1)
+
+            @pl.when((col != first) & (q >= 0) & (q < chunks))
             def _():
                 sum_copy(side, q, got.at[side, q], any_peer).wait_recv()
                 total = got[side, q].astype(jnp.float32) + sums[:, rows_of(side, q)].astype(
@@ -302,16 +324,23 @@
                     value = jax.nn.silu(total[0]) * total[1]
                     hidden[rows_of(side, q)] = value.astype(jnp.bfloat16)
                     hid_copy(side, q, up_peer).start()
-
-    for q in range(chunks):
+        return carry
+
+    def hid_step(step, carry):
         for side, (first, end, down_peer, up_peer) in enumerate(sides):
-            @pl.when(col != end)
+            q = step - (jnp.abs(col - end) - 1)
+
+            @pl.when((col != end) & (q >= 0) & (q < chunks))
             def _():
                 hid_copy(side, q, any_peer).wait_recv()
 
                 @pl.when(col != first)
                 def _():
                     hid_copy(side, q, up_peer).start()
+        return carry
+
+    lax.fori_loop(0, chunks + cols - 2, sum_step, 0)
+    lax.fori_loop(0, chunks + cols - 2, hid_step, 0)
 
     for q in range(chunks):
         for side, (first, end, down_peer, up_peer) in enumerate(sides):

time: 276 us -> 183 us (0.66)
  Pallas kernels: 272 us -> 179 us
    pallas_call x1, Pallas kernels: 178 us -> 97.4 us  [chain(): pl.pallas_call(functools.partial(chain_kernel, cols, chunks), in_specs=[V...]
    pallas_call x1, Pallas kernels: 37.5 us -> 25.2 us  [gather(): pl.pallas_call(functools.partial(gather_kernel, rows, cols, share), in_sp...]
where the time goes in v2:
time: 183 us; the launch traced here: 182 us
  Pallas kernels  179 us (98%)
  local copies, waits for them, and re-layouts  3.46 us (2%)
    pallas_call x1, Pallas kernels, chain(): pl.pallas_call(functools.partial(chain_kernel, cols, chunks), in_specs=[V...  97.4 us
    pallas_call x1, Pallas kernels, gather(): pl.pallas_call(functools.partial(gather_kernel, rows, cols, share), in_sp...  25.2 us
    pallas_call x1, Pallas kernels, project_up(): pl.pallas_call(up_kernel, grid=(width // tile,), in_specs=[pl.BlockSpec((...  23.7 us
    pallas_call x1, Pallas kernels, scatter(): pl.pallas_call(functools.partial(scatter_kernel, rows), in_specs=[VMEM_RE...  19.6 us
    pallas_call x1, Pallas kernels, project_down(): pl.pallas_call(down_kernel, grid=(width // tile,), in_specs=[pl.BlockSpec...  13 us

profile of v2, /device:TPU:0, one launch (start us, length us, event | category | flops | bytes accessed | tf_op | source)
XLA Modules:
  0.0 182.4 jit_solution(17437046346400138819)
XLA Ops:
  0.0 1.9 %reshape.3.down = bf16[8,28,1024]{2,1,0:T(8,128)(2,1)} reshape(bf16[224,1024]{1,0:T(8,128)(2,1)} %bitcast.1) | data formatting | bytes 917504 | tf_op jit(solution)/shard_map/reshape | solution.py:243
  1.9 25.2 %gather.1 = (bf16[256,2048]{1,0:T(8,128)(2,1)}, f32[16,3584]{1,0:T(8,128)}, f32[16,3584]{1,0:T(8,128)}, f32[28,2048]{1,0:T(8,128)}) custom-call(bf16[32,2048]{1,0:T(8,128)(2,1)} %tokens.1, bf16[8,28672]{1,0:T(8,128)(2,1)} %gate.2, bf16[8,28672]{1,0:T(8,128)(2,1)} %up.2, bf16[8,28,1024]{2,1,0:T(8,128)(2,1)} %reshape.3.down), custom_call_target="tpu_custom_call" | custom-call | tf_op jit(solution)/shard_map/gather/pallas_call | solution.py:244
  27.1 23.7 %shard_map.73.sums = bf16[2,256,3584]{2,1,0:T(8,128)(2,1)} custom-call(bf16[256,2048]{1,0:T(8,128)(2,1)} %get-tuple-element.9.tokens, s32[256,3584]{1,0:T(8,128)} %gate.3, s32[256,3584]{1,0:T(8,128)} %up.3, f32[16,3584]{1,0:T(8,128)} %get-tuple-element.10.gate_scale, f32[16,3584]{1,0:T(8,128)} %get-tuple-element.11.up_scale), custom_call_target="tpu_custom_call" | custom-call | flops 7516192768 | bytes 7340032 | tf_op jit(solution)/shard_map/pallas_call | solution.py:84
  50.8 97.4 %chain.1.hidden = bf16[256,3584]{1,0:T(8,128)(2,1)} custom-call(bf16[2,256,3584]{2,1,0:T(8,128)(2,1)} %shard_map.73.sums), custom_call_target="tpu_custom_call" | custom-call | tf_op jit(solution)/shard_map/chain/pallas_call | solution.py:362
  148.2 13.0 %shard_map.74.partial = bf16[256,2048]{1,0:T(8,128)(2,1)} custom-call(bf16[256,3584]{1,0:T(8,128)(2,1)} %chain.1.hidden, s32[448,2048]{1,0:T(8,128)} %codes.1, f32[28,2048]{1,0:T(8,128)} %get-tuple-element.12.scale), custom_call_target="tpu_custom_call" | custom-call | flops 3758096384 | bytes 3670016 | tf_op jit(solution)/shard_map/pallas_call | solution.py:108
  161.2 19.6 %scatter.1 = bf16[32,2048]{1,0:T(8,128)(2,1)} custom-call(bf16[256,2048]{1,0:T(8,128)(2,1)} %shard_map.74.partial), custom_call_target="tpu_custom_call" | custom-call | tf_op jit(solution)/shard_map/scatter/pallas_call | solution.py:410
  180.8 1.6 copy.9
